TPU v7x, 32 devices: a 4x2x2 block of a 4x4x8 slice. The times are simulated.
32 devices in a mesh: dp: 4 (over y, z), tp: 8 (over x, core).
Axes of the slice: x: 4, y: 2, z: 2, core: 2. Of those that a mesh axis runs over, the one named last changes fastest.
The devices are a block of a 4x4x8 slice.
Arguments:
- x: bfloat16 [1024, 2048], P(('dp', 'tp')), parts along dimension 0
- grad_y: bfloat16 [1024, 2048], P(('dp', 'tp')), parts along dimension 0
- gain_attn: float32 [2, 2048], replicated
- gain_mlp: float32 [2, 2048], replicated
- w_qkv: bfloat16 [2, 2048, 6144], P(None, None, 'tp')
- w_out: bfloat16 [2, 2048, 2048], P(None, 'tp')
- w_gate: bfloat16 [2, 2048, 8192], P(None, None, 'tp')
- w_up: bfloat16 [2, 2048, 8192], P(None, None, 'tp')
- w_down: bfloat16 [2, 8192, 2048], P(None, 'tp')
Outputs:
- output 1: bfloat16 [1024, 2048], P(('dp', 'tp')), parts along dimension 0
- output 2: bfloat16 [1024, 2048], P(('dp', 'tp')), parts along dimension 0
- output 3: bfloat16 [8, 2048, 6144], P('dp', None, 'tp'), parts along dimension 0
- output 4: bfloat16 [8, 2048, 2048], P('dp', 'tp'), parts along dimension 0
- output 5: bfloat16 [8, 2048, 8192], P('dp', None, 'tp'), parts along dimension 0
- output 6: bfloat16 [8, 2048, 8192], P('dp', None, 'tp'), parts along dimension 0
- output 7: bfloat16 [8, 8192, 2048], P('dp', 'tp'), parts along dimension 0
- output 8: float32 [8, 2048], P('dp'), parts along dimension 0
- output 9: float32 [8, 2048], P('dp'), parts along dimension 0
There are 4 independent parts. A program takes and returns all parts, laid end to end along the dimension named above; an argument that names none is the same for every part.
All inputs are finite; a program needn't handle non-finite values.
Results may differ from a plain program's by a relative error of at most 0.017051.
Values are sent between devices in bfloat16 or wider.
A program may use at most 768 MiB of HBM per device.

v0:
```python
import jax
import jax.numpy as jnp
from jax import lax
from jax.sharding import PartitionSpec as P

HEAD_DIM = 128
NORM_EPS = 1e-5


def rms_norm(hidden_in, gain_vec):
    hidden_f = hidden_in.astype(jnp.float32)
    inv_rms = lax.rsqrt(jnp.mean(hidden_f * hidden_f, axis=-1, keepdims=True) + NORM_EPS)
    return (hidden_f * inv_rms * gain_vec).astype(jnp.bfloat16)


def swiglu(gate_act, up_act):
    return (jax.nn.silu(gate_act.astype(jnp.float32)) * up_act.astype(jnp.float32)).astype(jnp.bfloat16)


def contract(left_op, right_op, eq_form):
    return jnp.einsum(eq_form, left_op, right_op, preferred_element_type=jnp.float32)


def gather_rows(row_shard):
    return lax.all_gather(row_shard, 'tp', axis=0, tiled=True)


def scatter_rows(part_sum):
    return lax.psum_scatter(part_sum, 'tp', scatter_dimension=0, tiled=True).astype(jnp.bfloat16)


def attention_core(full_in, w_qkv, kv_local, group_size):
    seq_len = full_in.shape[0]
    qkv_out = jnp.dot(full_in, w_qkv, preferred_element_type=jnp.float32).astype(jnp.bfloat16)
    blocks = qkv_out.reshape(seq_len, kv_local, group_size + 2, HEAD_DIM)
    queries = blocks[:, :, :group_size]
    key_rows = blocks[:, :, group_size]
    value_rows = blocks[:, :, group_size + 1]
    scores = contract(queries, key_rows, 'ikqh,jkh->kqij') * HEAD_DIM ** -0.5
    positions = jnp.arange(seq_len)
    causal = positions[:, None] >= positions[None, :]
    prob_f32 = jax.nn.softmax(jnp.where(causal, scores, -1e30), axis=-1)
    prob_low = prob_f32.astype(jnp.bfloat16)
    heads_out = contract(prob_low, value_rows, 'kqij,jkh->ikqh').astype(jnp.bfloat16)
    heads_out = heads_out.reshape(seq_len, kv_local * group_size * HEAD_DIM)
    return queries, key_rows, value_rows, prob_f32, prob_low, heads_out


def mlp_core(full_mid, w_gate, w_up):
    gate_act = jnp.dot(full_mid, w_gate, preferred_element_type=jnp.float32).astype(jnp.bfloat16)
    up_act = jnp.dot(full_mid, w_up, preferred_element_type=jnp.float32).astype(jnp.bfloat16)
    return gate_act, up_act, swiglu(gate_act, up_act)


def layer_forward(hidden_in, weights, kv_local, group_size):
    gain_attn, gain_mlp, w_qkv, w_out, w_gate, w_up, w_down = weights
    full_in = gather_rows(rms_norm(hidden_in, gain_attn))
    attn_parts = attention_core(full_in, w_qkv, kv_local, group_size)
    hidden_mid = hidden_in + scatter_rows(jnp.dot(attn_parts[5], w_out, preferred_element_type=jnp.float32))
    full_mid = gather_rows(rms_norm(hidden_mid, gain_mlp))
    mlp_parts = mlp_core(full_mid, w_gate, w_up)
    layer_out = hidden_mid + scatter_rows(jnp.dot(mlp_parts[2], w_down, preferred_element_type=jnp.float32))
    return layer_out, (full_in, attn_parts, hidden_mid, full_mid, mlp_parts)


def layer_backward(hidden_in, saved_acts, d_out, weights):
    gain_attn, gain_mlp, w_qkv, w_out, w_gate, w_up, w_down = weights
    full_in, attn_parts, hidden_mid, full_mid, mlp_parts = saved_acts
    queries, key_rows, value_rows, prob_f32, prob_low, heads_out = attn_parts
    gate_act, up_act, gated_act = mlp_parts
    seq_len, kv_local, group_size = queries.shape[0], queries.shape[1], queries.shape[2]
    d_down_full = gather_rows(d_out)
    grad_down = contract(gated_act, d_down_full, 'sf,sd->fd').astype(jnp.bfloat16)
    d_gated = contract(d_down_full, w_down, 'sd,fd->sf').astype(jnp.bfloat16)
    _, swiglu_pull = jax.vjp(swiglu, gate_act, up_act)
    d_gate, d_up = swiglu_pull(d_gated)
    grad_gate = contract(full_mid, d_gate, 'sd,sf->df').astype(jnp.bfloat16)
    grad_up = contract(full_mid, d_up, 'sd,sf->df').astype(jnp.bfloat16)
    d_mid = scatter_rows(contract(d_gate, w_gate, 'sf,df->sd') + contract(d_up, w_up, 'sf,df->sd'))
    _, norm_mid_pull = jax.vjp(rms_norm, hidden_mid, gain_mlp)
    d_norm_mid, grad_gain_mlp = norm_mid_pull(d_mid)
    d_hidden_mid = d_out + d_norm_mid
    d_attn_full = gather_rows(d_hidden_mid)
    grad_out = contract(heads_out, d_attn_full, 'sr,sd->rd').astype(jnp.bfloat16)
    d_heads = contract(d_attn_full, w_out, 'sd,rd->sr').astype(jnp.bfloat16).reshape(seq_len, kv_local, group_size, HEAD_DIM)
    d_prob = contract(d_heads, value_rows, 'ikqh,jkh->kqij')
    d_values = contract(prob_low, d_heads, 'kqij,ikqh->jkh').astype(jnp.bfloat16)
    d_scores = (prob_f32 * (d_prob - jnp.sum(d_prob * prob_f32, axis=-1, keepdims=True)) * HEAD_DIM ** -0.5).astype(jnp.bfloat16)
    d_queries = contract(d_scores, key_rows, 'kqij,jkh->ikqh').astype(jnp.bfloat16)
    d_keys = contract(d_scores, queries, 'kqij,ikqh->jkh').astype(jnp.bfloat16)
    d_qkv = jnp.concatenate([d_queries, d_keys[:, :, None], d_values[:, :, None]], axis=2).reshape(seq_len, -1)
    grad_qkv = contract(full_in, d_qkv, 'sd,sc->dc').astype(jnp.bfloat16)
    d_in = scatter_rows(contract(d_qkv, w_qkv, 'sc,dc->sd'))
    _, norm_in_pull = jax.vjp(rms_norm, hidden_in, gain_attn)
    d_norm_in, grad_gain_attn = norm_in_pull(d_in)
    return d_hidden_mid + d_norm_in, (grad_gain_attn, grad_gain_mlp, grad_qkv, grad_out, grad_gate, grad_up, grad_down)


def solution(mesh):
    row_spec = P(('dp', 'tp'), None)
    col_spec = P(None, None, 'tp')
    mid_spec = P(None, 'tp', None)
    in_specs = (row_spec, row_spec, P(None, None), P(None, None), col_spec, mid_spec, col_spec, col_spec, mid_spec)
    out_specs = (row_spec, row_spec, P('dp', None, 'tp'), P('dp', 'tp', None), P('dp', None, 'tp'), P('dp', None, 'tp'), P('dp', 'tp', None), P('dp', None), P('dp', None))

    def device_step(x, grad_y, gain_attn, gain_mlp, w_qkv, w_out, w_gate, w_up, w_down):
        all_weights = (gain_attn, gain_mlp, w_qkv, w_out, w_gate, w_up, w_down)
        num_layers = w_qkv.shape[0]
        rows_local = w_out.shape[1]
        kv_local = (w_qkv.shape[2] - rows_local) // (2 * HEAD_DIM)
        group_size = rows_local // (kv_local * HEAD_DIM)
        layer_inputs = [x]
        for layer_idx in range(num_layers):
            weights = tuple(weight[layer_idx] for weight in all_weights)
            layer_out, _ = layer_forward(layer_inputs[-1], weights, kv_local, group_size)
            layer_inputs.append(layer_out)
        d_hidden = grad_y
        layer_grads = [None] * num_layers
        for layer_idx in reversed(range(num_layers)):
            weights = tuple(weight[layer_idx] for weight in all_weights)
            kept_in, d_hidden = lax.optimization_barrier((layer_inputs[layer_idx], d_hidden))
            _, saved_acts = layer_forward(kept_in, weights, kv_local, group_size)
            d_hidden, layer_grads[layer_idx] = layer_backward(kept_in, saved_acts, d_hidden, weights)
        stacked = [jnp.stack([grads[kind_idx] for grads in layer_grads]) for kind_idx in range(7)]
        gain_grads = lax.psum(jnp.stack([stacked[0], stacked[1]]), 'tp')
        return (layer_inputs[-1], d_hidden, stacked[2], stacked[3], stacked[4], stacked[5], stacked[6], gain_grads[0], gain_grads[1])

    return jax.shard_map(device_step, mesh=mesh, in_specs=in_specs, out_specs=out_specs, check_vma=False)
```

profile of v0, /device:TPU:88, one launch (start us, length us, event | category | flops | bytes accessed | tf_op | source)
XLA Modules:
  0.0 677.3 jit_solution(3392537114868713828)
XLA Ops:
  9.1 1.7 fusion.216
  11.0 22.8 %all-gather.13.cloned.1.call-done = bf16[256,2048]{1,0:T(8,128)(2,1)} async-done(((bf16[32,2048]{1,0:T(8,128)(2,1)}), bf16[256,2048]{1,0:T(8,128)(2,1)}) %all-gather.13.cloned.1.call-update) | async-done | bytes 1048592 | tf_op jit(solution)/shard_map/all_gather | solution.py:25
  33.8 3.2 fusion.124
  37.8 1.8 fusion.180
  39.8 30.6 %reduce-scatter.11.cloned.1.call-done = f32[32,2048]{1,0:T(8,128)} async-done(((f32[256,2048]{1,0:T(8,128)}), f32[32,2048]{1,0:T(8,128)}) %reduce-scatter.11.cloned.1.call-update) | async-done | bytes 262160 | tf_op jit(solution)/shard_map/reduce_scatter | solution.py:29
  72.4 19.0 %all-gather.15.cloned.1.call-done = bf16[256,2048]{1,0:T(8,128)(2,1)} async-done(((bf16[32,2048]{1,0:T(8,128)(2,1)}), bf16[256,2048]{1,0:T(8,128)(2,1)}) %all-gather.15.cloned.1.call-update) | async-done | bytes 1048592 | tf_op jit(solution)/shard_map/all_gather | solution.py:25
  91.4 3.8 fusion.76
  95.2 7.5 %fusion.18 = f32[256,2048]{1,0:T(8,128)} fusion(bf16[2,1024,2048]{2,1,0:T(8,128)(2,1)} %param.17, bf16[256,2048]{1,0:T(8,128)(2,1)} %all-gather.15.cloned.1.call-done, bf16[2,2048,1024]{2,1,0:T(8,128)(2,1)} %param.16, bf16[256,1024]{1,0:T(8,128)(2,1)S(1)} %fusion.76), kind=kOutput, calls=%fused_computation.22 | convolution fusion | flops 2149842944 | bytes 12058624 | tf_op jit(solution)/shard_map/dot_general | solution.py:62
  102.8 30.7 %reduce-scatter.13.cloned.1.call-done = f32[32,2048]{1,0:T(8,128)} async-done(((f32[256,2048]{1,0:T(8,128)}), f32[32,2048]{1,0:T(8,128)}) %reduce-scatter.13.cloned.1.call-update) | async-done | bytes 262160 | tf_op jit(solution)/shard_map/reduce_scatter | solution.py:29
  136.3 18.9 %all-gather.23.cloned.1.call-done = bf16[256,2048]{1,0:T(8,128)(2,1)} async-done(((bf16[32,2048]{1,0:T(8,128)(2,1)}), bf16[256,2048]{1,0:T(8,128)(2,1)}) %all-gather.23.cloned.1.call-update) | async-done | bytes 1048592 | tf_op jit(solution)/shard_map/all_gather | solution.py:25
  155.1 3.2 fusion.133
  159.2 1.8 fusion.173
  161.9 29.8 %reduce-scatter.19.cloned.1.call-done = f32[32,2048]{1,0:T(8,128)} async-done(((f32[256,2048]{1,0:T(8,128)}), f32[32,2048]{1,0:T(8,128)}) %reduce-scatter.19.cloned.1.call-update) | async-done | bytes 262160 | tf_op jit(solution)/shard_map/reduce_scatter | solution.py:29
  194.2 17.9 %all-gather.21.cloned.1.call-done = bf16[256,2048]{1,0:T(8,128)(2,1)} async-done(((bf16[32,2048]{1,0:T(8,128)(2,1)}), bf16[256,2048]{1,0:T(8,128)(2,1)}) %all-gather.21.cloned.1.call-update) | async-done | bytes 1048592 | tf_op jit(solution)/shard_map/all_gather | solution.py:25
  212.2 4.6 fusion.121
  216.8 17.5 %all-gather.25.cloned.1.call-done = bf16[256,2048]{1,0:T(8,128)(2,1)} async-done(((bf16[32,2048]{1,0:T(8,128)(2,1)}), bf16[256,2048]{1,0:T(8,128)(2,1)}) %all-gather.25.cloned.1.call-update) | async-done | bytes 1048592 | tf_op jit(solution)/shard_map/all_gather | solution.py:25
  234.2 3.9 fusion.103
  238.2 3.8 fusion.4
  242.0 3.4 fusion.118
  246.3 2.9 fusion.65
  249.3 30.6 %reduce-scatter.21.cloned.1.call-done = f32[32,2048]{1,0:T(8,128)} async-done(((f32[256,2048]{1,0:T(8,128)}), f32[32,2048]{1,0:T(8,128)}) %reduce-scatter.21.cloned.1.call-update) | async-done | bytes 262160 | tf_op jit(solution)/shard_map/reduce_scatter | solution.py:29
  282.3 1.8 fusion.253
  284.2 18.9 %all-gather.27.cloned.1.call-done = bf16[256,2048]{1,0:T(8,128)(2,1)} async-done(((bf16[32,2048]{1,0:T(8,128)(2,1)}), bf16[256,2048]{1,0:T(8,128)(2,1)}) %all-gather.27.cloned.1.call-update) | async-done | bytes 1048592 | tf_op jit(solution)/shard_map/all_gather | solution.py:25
  303.1 1.7 convolution_convert_fusion.15
  307.5 4.3 fusion.48
  311.9 30.7 %reduce-scatter.23.cloned.1.call-done = f32[32,2048]{1,0:T(8,128)} async-done(((f32[256,2048]{1,0:T(8,128)}), f32[32,2048]{1,0:T(8,128)}) %reduce-scatter.23.cloned.1.call-update) | async-done | bytes 262160 | tf_op jit(solution)/shard_map/reduce_scatter | solution.py:29
  342.7 2.3 fusion.227
  345.0 1.8 fusion.252
  347.9 18.9 %all-gather.31.cloned.1.call-done = bf16[256,2048]{1,0:T(8,128)(2,1)} async-done(((bf16[32,2048]{1,0:T(8,128)(2,1)}), bf16[256,2048]{1,0:T(8,128)(2,1)}) %all-gather.31.cloned.1.call-update) | async-done | bytes 1048592 | tf_op jit(solution)/shard_map/all_gather | solution.py:25
  366.7 3.2 fusion.127
  371.4 1.8 fusion.178
  374.7 29.3 %reduce-scatter.25.cloned.1.call-done = f32[32,2048]{1,0:T(8,128)} async-done(((f32[256,2048]{1,0:T(8,128)}), f32[32,2048]{1,0:T(8,128)}) %reduce-scatter.25.cloned.1.call-update) | async-done | bytes 262160 | tf_op jit(solution)/shard_map/reduce_scatter | solution.py:29
  406.2 18.7 %all-gather.17.cloned.1.call-done = bf16[256,2048]{1,0:T(8,128)(2,1)} async-done(((bf16[32,2048]{1,0:T(8,128)(2,1)}), bf16[256,2048]{1,0:T(8,128)(2,1)}) %all-gather.17.cloned.1.call-update) | async-done | bytes 1048592 | tf_op jit(solution)/shard_map/all_gather | solution.py:25
  424.9 3.9 fusion.130
  430.6 1.8 fusion.175
  432.5 14.2 %all-gather.29.cloned.1.call-done = bf16[256,2048]{1,0:T(8,128)(2,1)} async-done(((bf16[32,2048]{1,0:T(8,128)(2,1)}), bf16[256,2048]{1,0:T(8,128)(2,1)}) %all-gather.29.cloned.1.call-update) | async-done | bytes 1048592 | tf_op jit(solution)/shard_map/all_gather | solution.py:25
  446.8 3.8 fusion.97
  450.6 18.1 %all-gather.33.cloned.1.call-done = bf16[256,2048]{1,0:T(8,128)(2,1)} async-done(((bf16[32,2048]{1,0:T(8,128)(2,1)}), bf16[256,2048]{1,0:T(8,128)(2,1)}) %all-gather.33.cloned.1.call-update) | async-done | bytes 1048592 | tf_op jit(solution)/shard_map/all_gather | solution.py:25
  468.7 3.8 fusion.79
  472.6 3.7 fusion.94
  476.3 3.8 fusion.20
  480.2 4.0 fusion.62
  484.3 17.8 %reduce-scatter.15.cloned.1.call-done = f32[32,2048]{1,0:T(8,128)} async-done(((f32[256,2048]{1,0:T(8,128)}), f32[32,2048]{1,0:T(8,128)}) %reduce-scatter.15.cloned.1.call-update) | async-done | bytes 262160 | tf_op jit(solution)/shard_map/reduce_scatter | solution.py:29
  504.1 30.3 %reduce-scatter.27.cloned.1.call-done = f32[32,2048]{1,0:T(8,128)} async-done(((f32[256,2048]{1,0:T(8,128)}), f32[32,2048]{1,0:T(8,128)}) %reduce-scatter.27.cloned.1.call-update) | async-done | bytes 262160 | tf_op jit(solution)/shard_map/reduce_scatter | solution.py:29
  535.6 1.7 fusion.251
  537.5 18.0 %all-gather.19.cloned.1.call-done = bf16[256,2048]{1,0:T(8,128)(2,1)} async-done(((bf16[32,2048]{1,0:T(8,128)(2,1)}), bf16[256,2048]{1,0:T(8,128)(2,1)}) %all-gather.19.cloned.1.call-update) | async-done | bytes 1048592 | tf_op jit(solution)/shard_map/all_gather | solution.py:25
  555.5 4.6 fusion.100
  560.1 7.7 %fusion.2 = f32[256,2048]{1,0:T(8,128)} fusion(bf16[2,1024,2048]{2,1,0:T(8,128)(2,1)} %param.17, bf16[256,2048]{1,0:T(8,128)(2,1)} %all-gather.19.cloned.1.call-done, bf16[2,2048,1024]{2,1,0:T(8,128)(2,1)} %param.16, bf16[256,1024]{1,0:T(8,128)(2,1)} %fusion.100), kind=kOutput, calls=%fused_computation.6 | convolution fusion | flops 2149842944 | bytes 12058624 | tf_op jit(solution)/shard_map/dot_general | solution.py:62
  568.1 5.1 convert_bitcast_fusion
  573.3 3.4 convert_bitcast_fusion.2
  576.7 3.5 convert_bitcast_fusion.4
  580.2 1.7 convolution_convert_fusion.14
  583.2 4.5 fusion.54
  588.2 4.0 fusion.61
  592.3 3.5 convert_bitcast_fusion.1
  595.7 3.5 convert_bitcast_fusion.3
  599.2 3.8 convert_bitcast_fusion.5
  603.0 6.3 pad_maximum_fusion.2
  609.4 11.6 %pad_maximum_fusion = (bf16[2,2048,1024]{2,1,0:T(8,128)(2,1)}, bf16[2,2048,1024]{2,1,0:T(8,128)(2,1)}) fusion(bf16[1,2048,1024]{2,1,0:T(8,128)(2,1)} %convert_bitcast_fusion.4, bf16[1,2048,1024]{2,1,0:T(8,128)(2,1)} %convert_bitcast_fusion.5, bf16[1,2048,1024]{2,1,0:T(8,128)(2,1)} %convert_bitcast_fusion.2, bf16[1,2048,1024]{2,1,0:T(8,128)(2,1)} %convert_bitcast_fusion.3), kind=kLoop, calls=%fused_computation | loop fusion | flops 8388608 | bytes 33554432 | tf_op jit(solution)/shard_map/stack | solution.py:124
  624.3 2.4 fusion.60
  628.3 3.2 pad_maximum_fusion.3
  631.5 10.9 %reduce-scatter.29.cloned.1.call-done = f32[32,2048]{1,0:T(8,128)} async-done(((f32[256,2048]{1,0:T(8,128)}), f32[32,2048]{1,0:T(8,128)}) %reduce-scatter.29.cloned.1.call-update) | async-done | bytes 262160 | tf_op jit(solution)/shard_map/reduce_scatter | solution.py:29
  643.7 24.0 %psum.7 = f32[2,2,2048]{2,1,0:T(2,128)S(1)} all-reduce(f32[2,2,2048]{2,1,0:T(2,128)S(1)} %pad_maximum_fusion.7), channel_id=1, replica_groups=mesh['dp'=4,'tp'=8] {'tp'}, use_global_device_ids=true, to_apply=%region_36.37 | all-reduce | flops 8192 | bytes 65536 | tf_op jit(solution)/shard_map/psum | solution.py:125
  668.2 1.7 fusion.250
  (261 shorter events, 38.2 us)
Async XLA Ops:
  7.2 26.6 %all-gather.13.cloned.1.call-start = ((), (), s32[]{:S(2)}) async-start(), calls=%async_computation.10 | async-start | bytes 1179648 | tf_op jit(solution)/shard_map/all_gather | solution.py:25
  8.1 127.3 %copy-start.21 = (f32[1,2048]{1,0:T(1,128)}, f32[1,2048]{1,0:T(1,128)S(1)}, u32[]{:S(2)}) copy-start(f32[1,2048]{1,0:T(1,128)S(1)} %get-tuple-element.39) | copy-start | bytes 24580
  10.9 59.5 %reduce-scatter.11.cloned.1.call-start = ((), (), s32[]{:S(2)}) async-start(), calls=%async_computation.11 | async-start | bytes 2359296 | tf_op jit(solution)/shard_map/reduce_scatter | solution.py:29
  11.0 147.5 %copy-start.23 = (pred[256,256]{0,1:T(8,128)(4,1)}, pred[256,256]{0,1:T(8,128)(4,1)S(1)}, u32[]{:S(2)}) copy-start(pred[256,256]{0,1:T(8,128)(4,1)S(1)} %iota_compare_fusion) | copy-start | bytes 196612
  11.0 26.8 %copy-start = (bf16[2,256,2048]{2,1,0:T(8,128)(2,1)S(1)}, bf16[2,256,2048]{2,1,0:T(8,128)(2,1)}, u32[]{:S(2)}) copy-start(bf16[2,256,2048]{2,1,0:T(8,128)(2,1)} %param.14) | copy-start | bytes 6291460
  37.4 32.9 %copy-start.1 = (bf16[32,2048]{1,0:T(8,128)(2,1)S(1)}, bf16[32,2048]{1,0:T(8,128)(2,1)}, u32[]{:S(2)}) copy-start(bf16[32,2048]{1,0:T(8,128)(2,1)} %param.9) | copy-start | bytes 393220
  39.6 51.7 %all-gather.15.cloned.1.call-start = ((), (), s32[]{:S(2)}) async-start(), calls=%async_computation.12 | async-start | bytes 1179648 | tf_op jit(solution)/shard_map/all_gather | solution.py:25
  39.8 153.1 %copy-start.19 = (f32[1,2048]{1,0:T(1,128)}, f32[1,2048]{1,0:T(1,128)S(1)}, u32[]{:S(2)}) copy-start(f32[1,2048]{1,0:T(1,128)S(1)} %get-tuple-element.37) | copy-start | bytes 24580
  72.3 61.3 %reduce-scatter.13.cloned.1.call-start = ((), (), s32[]{:S(2)}) async-start(), calls=%async_computation.13 | async-start | bytes 2359296 | tf_op jit(solution)/shard_map/reduce_scatter | solution.py:29
  102.8 52.4 %all-gather.23.cloned.1.call-start = ((), (), s32[]{:S(2)}) async-start(), calls=%async_computation.19 | async-start | bytes 1179648 | tf_op jit(solution)/shard_map/all_gather | solution.py:25
  135.3 23.5 %copy-start.45 = (f32[32]{0:T(128)}, f32[32]{0:T(128)S(1)}, u32[]{:S(2)}) copy-start(f32[32]{0:T(128)S(1)} %fusion.234) | copy-start | bytes 388
  135.3 23.4 %copy-start.38 = (f32[32]{0:T(128)}, f32[32]{0:T(128)S(1)}, u32[]{:S(2)}) copy-start(f32[32]{0:T(128)S(1)} %fusion.258) | copy-start | bytes 388
  136.2 55.6 %reduce-scatter.19.cloned.1.call-start = ((), (), s32[]{:S(2)}) async-start(), calls=%async_computation.20 | async-start | bytes 2359296 | tf_op jit(solution)/shard_map/reduce_scatter | solution.py:29
  158.8 34.0 %copy-start.32 = (f32[2,256]{1,0:T(2,128)}, f32[2,256]{1,0:T(2,128)S(1)}, u32[]{:S(2)}) copy-start(f32[2,256]{1,0:T(2,128)S(1)} %get-tuple-element.44) | copy-start | bytes 6148
  158.9 34.7 %copy-start.34 = (f32[2,256]{1,0:T(2,128)}, f32[2,256]{1,0:T(2,128)S(1)}, u32[]{:S(2)}) copy-start(f32[2,256]{1,0:T(2,128)S(1)} %fusion.199) | copy-start | bytes 6148
  161.0 51.2 %all-gather.21.cloned.1.call-start = ((), (), s32[]{:S(2)}) async-start(), calls=%async_computation.18 | async-start | bytes 1179648 | tf_op jit(solution)/shard_map/all_gather | solution.py:25
  161.8 72.4 %all-gather.25.cloned.1.call-start = ((), (), s32[]{:S(2)}) async-start(), calls=%async_computation.21 | async-start | bytes 1179648 | tf_op jit(solution)/shard_map/all_gather | solution.py:25
  192.8 23.9 %copy-start.50 = (f32[32]{0:T(128)}, f32[32]{0:T(128)S(1)}, u32[]{:S(2)}) copy-start(f32[32]{0:T(128)S(1)} %get-tuple-element.27) | copy-start | bytes 388
  192.9 23.9 %copy-start.42 = (f32[32]{0:T(128)}, f32[32]{0:T(128)S(1)}, u32[]{:S(2)}) copy-start(f32[32]{0:T(128)S(1)} %fusion.259) | copy-start | bytes 388
  193.7 86.3 %reduce-scatter.21.cloned.1.call-start = ((), (), s32[]{:S(2)}) async-start(), calls=%async_computation.22 | async-start | bytes 2359296 | tf_op jit(solution)/shard_map/reduce_scatter | solution.py:29
  234.2 12.0 %slice-start = ((s8[8388608]{0:T(1024)(128)(4,1)}), s8[4194304]{0:T(1024)(128)(4,1)S(1)}, s32[]{:S(2)}) async-start(s8[8388608]{0:T(1024)(128)(4,1)} %bitcast.423), calls=%async_computation.32 | async-start | bytes 8388608
  238.2 7.3 %copy-start.58 = (bf16[256,1024]{1,0:T(8,128)(2,1)}, bf16[256,1024]{1,0:T(8,128)(2,1)S(1)}, u32[]{:S(2)}) copy-start(bf16[256,1024]{1,0:T(8,128)(2,1)S(1)} %fusion.103) | copy-start | bytes 1572868
  238.2 8.1 %slice-start.1 = ((s8[8388608]{0:T(1024)(128)(4,1)}), s8[4194304]{0:T(1024)(128)(4,1)S(1)}, s32[]{:S(2)}) async-start(s8[8388608]{0:T(1024)(128)(4,1)} %bitcast.423), calls=%async_computation.33 | async-start | bytes 8388608
  246.3 36.0 %copy-start.14 = (bf16[32,2048]{1,0:T(8,128)(2,1)S(1)}, bf16[32,2048]{1,0:T(8,128)(2,1)}, u32[]{:S(2)}) copy-start(bf16[32,2048]{1,0:T(8,128)(2,1)} %param.10) | copy-start | bytes 393220
  249.2 53.8 %all-gather.27.cloned.1.call-start = ((), (), s32[]{:S(2)}) async-start(), calls=%async_computation.23 | async-start | bytes 1179648 | tf_op jit(solution)/shard_map/all_gather | solution.py:25
  284.1 21.6 %copy-start.33 = (f32[2,256]{1,0:T(2,128)S(1)}, f32[2,256]{1,0:T(2,128)}, u32[]{:S(2)}) copy-start(f32[2,256]{1,0:T(2,128)} %copy-done.32) | copy-start | bytes 6148
  284.1 21.7 %copy-start.35 = (f32[2,256]{1,0:T(2,128)S(1)}, f32[2,256]{1,0:T(2,128)}, u32[]{:S(2)}) copy-start(f32[2,256]{1,0:T(2,128)} %copy-done.34) | copy-start | bytes 6148
  284.1 58.5 %reduce-scatter.23.cloned.1.call-start = ((), (), s32[]{:S(2)}) async-start(), calls=%async_computation.24 | async-start | bytes 2359296 | tf_op jit(solution)/shard_map/reduce_scatter | solution.py:29
  306.7 36.0 %copy-start.22 = (f32[1,2048]{1,0:T(1,128)S(1)}, f32[1,2048]{1,0:T(1,128)}, u32[]{:S(2)}) copy-start(f32[1,2048]{1,0:T(1,128)} %copy-done.21) | copy-start | bytes 24580
  306.7 36.0 %copy-start.39 = (f32[32]{0:T(128)S(1)}, f32[32]{0:T(128)}, u32[]{:S(2)}) copy-start(f32[32]{0:T(128)} %copy-done.38) | copy-start | bytes 388
  307.5 37.5 %copy-start.46 = (f32[32]{0:T(128)S(1)}, f32[32]{0:T(128)}, u32[]{:S(2)}) copy-start(f32[32]{0:T(128)} %copy-done.45) | copy-start | bytes 388
  307.5 37.5 %copy-start.6 = (bf16[32,2048]{1,0:T(8,128)(2,1)S(1)}, bf16[32,2048]{1,0:T(8,128)(2,1)}, u32[]{:S(2)}) copy-start(bf16[32,2048]{1,0:T(8,128)(2,1)} %fusion.253) | copy-start | bytes 393220
  311.8 54.9 %all-gather.31.cloned.1.call-start = ((), (), s32[]{:S(2)}) async-start(), calls=%async_computation.26 | async-start | bytes 1179648 | tf_op jit(solution)/shard_map/all_gather | solution.py:25
  345.0 25.1 %copy-start.24 = (pred[256,256]{0,1:T(8,128)(4,1)S(1)}, pred[256,256]{0,1:T(8,128)(4,1)}, u32[]{:S(2)}) copy-start(pred[256,256]{0,1:T(8,128)(4,1)} %copy-done.23) | copy-start | bytes 196612
  346.9 23.5 %copy-start.43 = (f32[32]{0:T(128)}, f32[32]{0:T(128)S(1)}, u32[]{:S(2)}) copy-start(f32[32]{0:T(128)S(1)} %fusion.238) | copy-start | bytes 388
  347.0 23.1 %copy-start.36 = (f32[32]{0:T(128)}, f32[32]{0:T(128)S(1)}, u32[]{:S(2)}) copy-start(f32[32]{0:T(128)S(1)} %fusion.260) | copy-start | bytes 388
  347.8 56.2 %reduce-scatter.25.cloned.1.call-start = ((), (), s32[]{:S(2)}) async-start(), calls=%async_computation.27 | async-start | bytes 2359296 | tf_op jit(solution)/shard_map/reduce_scatter | solution.py:29
  370.5 34.6 %copy-start.30 = (f32[2,256]{1,0:T(2,128)}, f32[2,256]{1,0:T(2,128)S(1)}, u32[]{:S(2)}) copy-start(f32[2,256]{1,0:T(2,128)S(1)} %fusion.201) | copy-start | bytes 6148
  373.3 51.6 %all-gather.17.cloned.1.call-start = ((), (), s32[]{:S(2)}) async-start(), calls=%async_computation.14 | async-start | bytes 1179648 | tf_op jit(solution)/shard_map/all_gather | solution.py:25
  373.9 72.8 %all-gather.29.cloned.1.call-start = ((), (), s32[]{:S(2)}) async-start(), calls=%async_computation.25 | async-start | bytes 1179648 | tf_op jit(solution)/shard_map/all_gather | solution.py:25
  374.6 94.1 %all-gather.33.cloned.1.call-start = ((), (), s32[]{:S(2)}) async-start(), calls=%async_computation.28 | async-start | bytes 1179648 | tf_op jit(solution)/shard_map/all_gather | solution.py:25
  405.1 25.2 %copy-start.48 = (f32[32]{0:T(128)}, f32[32]{0:T(128)S(1)}, u32[]{:S(2)}) copy-start(f32[32]{0:T(128)S(1)} %get-tuple-element.25) | copy-start | bytes 388
  405.1 25.2 %copy-start.40 = (f32[32]{0:T(128)}, f32[32]{0:T(128)S(1)}, u32[]{:S(2)}) copy-start(f32[32]{0:T(128)S(1)} %fusion.261) | copy-start | bytes 388
  406.0 96.1 %reduce-scatter.15.cloned.1.call-start = ((), (), s32[]{:S(2)}) async-start(), calls=%async_computation.15 | async-start | bytes 2359296 | tf_op jit(solution)/shard_map/reduce_scatter | solution.py:29
  432.5 101.9 %reduce-scatter.27.cloned.1.call-start = ((), (), s32[]{:S(2)}) async-start(), calls=%async_computation.29 | async-start | bytes 2359296 | tf_op jit(solution)/shard_map/reduce_scatter | solution.py:29
  450.6 25.7 %copy-start.62 = (bf16[256,1024]{1,0:T(8,128)(2,1)}, bf16[256,1024]{1,0:T(8,128)(2,1)S(1)}, u32[]{:S(2)}) copy-start(bf16[256,1024]{1,0:T(8,128)(2,1)S(1)} %fusion.97) | copy-start | bytes 1572868
  472.5 7.5 %copy-start.64 = (bf16[256,1024]{1,0:T(8,128)(2,1)}, bf16[256,1024]{1,0:T(8,128)(2,1)S(1)}, u32[]{:S(2)}) copy-start(bf16[256,1024]{1,0:T(8,128)(2,1)S(1)} %fusion.79) | copy-start | bytes 1572868
  472.6 7.6 %slice-start.2 = ((s8[8388608]{0:T(1024)(128)(4,1)}), s8[4194304]{0:T(1024)(128)(4,1)S(1)}, s32[]{:S(2)}) async-start(s8[8388608]{0:T(1024)(128)(4,1)} %bitcast.425), calls=%async_computation.34 | async-start | bytes 8388608
  480.1 23.1 %copy-start.20 = (f32[1,2048]{1,0:T(1,128)S(1)}, f32[1,2048]{1,0:T(1,128)}, u32[]{:S(2)}) copy-start(f32[1,2048]{1,0:T(1,128)} %copy-done.19) | copy-start | bytes 24580
  480.2 54.3 %copy-start.41 = (f32[32]{0:T(128)S(1)}, f32[32]{0:T(128)}, u32[]{:S(2)}) copy-start(f32[32]{0:T(128)} %copy-done.40) | copy-start | bytes 388
  480.2 55.4 %copy-start.49 = (f32[32]{0:T(128)S(1)}, f32[32]{0:T(128)}, u32[]{:S(2)}) copy-start(f32[32]{0:T(128)} %copy-done.48) | copy-start | bytes 388
  480.2 55.4 %copy-start.4 = (bf16[32,2048]{1,0:T(8,128)(2,1)S(1)}, bf16[32,2048]{1,0:T(8,128)(2,1)}, u32[]{:S(2)}) copy-start(bf16[32,2048]{1,0:T(8,128)(2,1)} %fusion.252) | copy-start | bytes 393220
  484.2 71.3 %all-gather.19.cloned.1.call-start = ((), (), s32[]{:S(2)}) async-start(), calls=%async_computation.16 | async-start | bytes 1179648 | tf_op jit(solution)/shard_map/all_gather | solution.py:25
  504.0 76.2 %all-gather.35.cloned.1.call-start = ((), (), s32[]{:S(2)}) async-start(), calls=%async_computation.30 | async-start | bytes 1179648 | tf_op jit(solution)/shard_map/all_gather | solution.py:25
  537.4 83.6 %reduce-scatter.17.cloned.1.call-start = ((), (), s32[]{:S(2)}) async-start(), calls=%async_computation.17 | async-start | bytes 2359296 | tf_op jit(solution)/shard_map/reduce_scatter | solution.py:29
  567.8 74.5 %reduce-scatter.29.cloned.1.call-start = ((), (), s32[]{:S(2)}) async-start(), calls=%async_computation.31 | async-start | bytes 2359296 | tf_op jit(solution)/shard_map/reduce_scatter | solution.py:29
  576.7 5.2 copy-start.31
  609.3 13.3 %copy-start.13 = (bf16[2,128,256]{2,1,0:T(8,128)(2,1)S(1)}, bf16[2,128,256]{2,1,0:T(8,128)(2,1)}, u32[]{:S(2)}) copy-start(bf16[2,128,256]{2,1,0:T(8,128)(2,1)} %copy-done.12) | copy-start | bytes 393220
  609.4 14.9 %copy-start.18 = (bf16[256,2,3,128]{0,3,2,1:T(8,128)(2,1)S(1)}, bf16[256,2,3,128]{0,3,2,1:T(8,128)(2,1)}, u32[]{:S(2)}) copy-start(bf16[256,2,3,128]{0,3,2,1:T(8,128)(2,1)} %copy-done.17) | copy-start | bytes 1179652
  628.2 14.1 %copy-start.37 = (f32[32]{0:T(128)S(1)}, f32[32]{0:T(128)}, u32[]{:S(2)}) copy-start(f32[32]{0:T(128)} %copy-done.36) | copy-start | bytes 388
  628.2 15.3 %copy-start.44 = (f32[32]{0:T(128)S(1)}, f32[32]{0:T(128)}, u32[]{:S(2)}) copy-start(f32[32]{0:T(128)} %copy-done.43) | copy-start | bytes 388
  628.2 15.3 %copy-start.25 = (f32[2048]{0:T(1024)S(1)}, f32[2048]{0:T(1024)}, u32[]{:S(2)}) copy-start(f32[2048]{0:T(1024)} %get-tuple-element.19) | copy-start | bytes 24580
  628.2 15.3 %copy-start.26 = (f32[2048]{0:T(1024)S(1)}, f32[2048]{0:T(1024)}, u32[]{:S(2)}) copy-start(f32[2048]{0:T(1024)} %get-tuple-element.23) | copy-start | bytes 24580
  628.3 40.0 %copy-start.5 = (bf16[32,2048]{1,0:T(8,128)(2,1)S(1)}, bf16[32,2048]{1,0:T(8,128)(2,1)}, u32[]{:S(2)}) copy-start(bf16[32,2048]{1,0:T(8,128)(2,1)} %fusion.251) | copy-start | bytes 393220
  (30 other events, 116.0 us)
Sparse Core Ops, SparseCore 0:
  11.0 22.7 all-gather.12
  39.8 30.5 reduce-scatter.10
  72.6 18.7 all-gather.14
  102.9 30.6 reduce-scatter.12
  136.3 18.7 all-gather.22
  161.1 30.5 reduce-scatter.18
  193.4 18.7 all-gather.20
  214.4 19.8 all-gather.24
  249.4 30.5 reduce-scatter.20
  284.3 18.7 all-gather.26
  311.9 30.6 reduce-scatter.22
  347.9 18.7 all-gather.30
  373.4 30.5 reduce-scatter.24
  406.1 18.7 all-gather.16
  426.9 19.8 all-gather.28
  448.8 19.8 all-gather.32
  471.4 30.6 reduce-scatter.14
  504.8 29.5 reduce-scatter.26
  536.6 18.8 all-gather.18
  557.0 19.8 all-gather.34
  579.7 30.6 reduce-scatter.16
  612.7 29.6 reduce-scatter.28
where the time goes:
time: 684 us; the launch traced here: 677 us
  waiting for transfers between devices  447 us (65%)
  matrix products  130 us (19%)
  other arithmetic  52.8 us (8%)
  blocking collectives  24 us (4%)
  between operations  16 us (2%)
    reduce_scatter x10, waiting for transfers between devices, scatter_rows(): lax.psum_scatter(part_sum, 'tp', scatter_dimension=0, tiled=True)  241 us
    all_gather x12, waiting for transfers between devices, gather_rows(): return lax.all_gather(row_shard, 'tp', axis=0, tiled=True)  203 us
    dot_general x36, matrix products, contract(): jnp.einsum(eq_form, left_op, right_op, preferred_element_type=jnp.float32)  70.9 us
    psum x1, blocking collectives, device_step(): gain_grads = lax.psum(jnp.stack([stacked[0], stacked[1]]), 'tp')  24 us
    another operation x4, other arithmetic, device_step(): jnp.stack([grads[kind_idx] for grads in layer_grads])  22.7 us
    dot_general x4, matrix products, mlp_core(): jnp.dot(full_mid, w_gate, preferred_element_type=jnp.float32)  16.1 us
    dot_general x2, matrix products, layer_forward(): jnp.dot(mlp_parts[2], w_down, preferred_element_type=jnp.float32)  15.2 us
  transfers between devices with their start and end apart: 22, of which 20 were waited for; matrix products, arithmetic and copies ran while one was open for 17% of the time, Pallas kernels for 0%

commit v1 on v0

v1 whole, which is shorter than its diff:
```python
import functools

import jax
import jax.numpy as jnp
from jax import lax
from jax.experimental import pallas as pl
from jax.experimental.pallas import tpu as pltpu
from jax.sharding import PartitionSpec as P

HEAD_DIM = 128
NORM_EPS = 1e-5
BF = jnp.bfloat16
F32 = jnp.float32
CHUNKS = 4
VMEM_LIMIT = 62 * 1024 * 1024


def dot_nn(a, b):
    return lax.dot_general(a, b, (((1,), (0,)), ((), ())), preferred_element_type=F32)


def dot_nt(a, b):
    return lax.dot_general(a, b, (((1,), (1,)), ((), ())), preferred_element_type=F32)


def dot_tn(a, b):
    return lax.dot_general(a, b, (((0,), (0,)), ((), ())), preferred_element_type=F32)


def norm(h, gain):
    hf = h.astype(F32)
    inv = lax.rsqrt(jnp.mean(hf * hf, axis=-1, keepdims=True) + NORM_EPS)
    return (hf * inv * gain).astype(BF)


def norm_grad(h, gain, dy):
    hf = h.astype(F32)
    dyf = dy.astype(F32)
    inv = lax.rsqrt(jnp.mean(hf * hf, axis=-1, keepdims=True) + NORM_EPS)
    hn = hf * inv
    dgain = jnp.sum(dyf * hn, axis=0, keepdims=True)
    gdy = dyf * gain
    dh = inv * (gdy - hn * jnp.mean(gdy * hn, axis=-1, keepdims=True))
    return dh.astype(BF), dgain


class Place:
    def __init__(self, n):
        self.n = n
        self.me = lax.axis_index('tp')
        self.side = lax.rem(self.me, 2)
        self.chip = self.me // 2
        nc = n // 2
        self.lchip = lax.rem(self.chip + nc - 1, nc)
        self.rchip = lax.rem(self.chip + 1, nc)
        self.ochip = lax.rem(self.chip + 2, nc)
        self.partner = self.chip * 2 + 1 - self.side
        self.left = self.lchip * 2 + self.side
        self.right = self.rchip * 2 + self.side
        self.opp = self.ochip * 2 + self.side
        self.pleft = self.lchip * 2 + 1 - self.side
        self.pright = self.rchip * 2 + 1 - self.side
        self.popp = self.ochip * 2 + 1 - self.side

    def barrier(self, everyone=False):
        sem = pltpu.get_barrier_semaphore()
        if everyone:
            for k in range(1, self.n):
                pl.semaphore_signal(sem, inc=1, device_id={'tp': lax.rem(self.me + k, self.n)},
                                    device_id_type=pl.DeviceIdType.MESH)
            pl.semaphore_wait(sem, self.n - 1)
        else:
            for peer in (self.partner, self.left, self.right):
                pl.semaphore_signal(sem, inc=1, device_id={'tp': peer}, device_id_type=pl.DeviceIdType.MESH)
            pl.semaphore_wait(sem, 3)


def remote(src, dst, ssem, rsem, peer):
    return pltpu.make_async_remote_copy(src_ref=src, dst_ref=dst, send_sem=ssem, recv_sem=rsem,
                                        device_id={'tp': peer}, device_id_type=pl.DeviceIdType.MESH)


class Gather:
    def __init__(self, place, buf, ssem, rsem):
        self.p, self.buf, self.ssem, self.rsem = place, buf, ssem, rsem
        self.rows = buf.shape[0] // place.n
        self.half = self.rows // 2
        self.sent = []

    def view(self, shard, part):
        if part is None:
            return self.buf.at[pl.ds(pl.multiple_of(shard * self.rows, self.rows), self.rows), :]
        return self.buf.at[pl.ds(pl.multiple_of(shard * self.rows + part * self.half, self.half), self.half), :]

    def send(self, k, peer, shard, part):
        v = self.view(shard, part)
        cp = remote(v, v, self.ssem.at[k], self.rsem.at[k], peer)
        cp.start()
        self.sent.append(cp)

    def recv(self, k, shard, part):
        v = self.view(shard, part)
        remote(v, v, self.ssem.at[k], self.rsem.at[k], self.p.partner).wait_recv()

    def start(self):
        p = self.p
        self.send(1, p.right, p.me, 0)
        self.send(3, p.left, p.me, 1)
        self.send(2, p.right, p.me, 1)
        self.send(4, p.left, p.me, 0)
        self.send(0, p.partner, p.me, None)

    def finish(self):
        p = self.p
        self.recv(1, p.left, 0)
        self.send(5, p.right, p.left, 0)
        self.send(7, p.partner, p.left, 0)
        self.recv(3, p.right, 1)
        self.send(6, p.left, p.right, 1)
        self.send(8, p.partner, p.right, 1)
        self.recv(2, p.left, 1)
        self.send(9, p.partner, p.left, 1)
        self.recv(4, p.right, 0)
        self.send(10, p.partner, p.right, 0)
        self.recv(5, p.opp, 0)
        self.send(11, p.partner, p.opp, 0)
        self.recv(6, p.opp, 1)
        self.send(12, p.partner, p.opp, 1)
        self.recv(0, p.partner, None)
        self.recv(7, p.pleft, 0)
        self.recv(8, p.pright, 1)
        self.recv(9, p.pleft, 1)
        self.recv(10, p.pright, 0)
        self.recv(11, p.popp, 0)
        self.recv(12, p.popp, 1)
        for cp in self.sent:
            cp.wait_send()
        self.sent = []


class Scatter:
    def __init__(self, place, part, pair, froml, fromr, dsem, rsem):
        self.p = place
        self.part, self.pair, self.froml, self.fromr = part, pair, froml, fromr
        self.dsem, self.rsem = dsem, rsem
        self.rows, self.cols = part.shape[3], part.shape[4]
        self.half = self.rows // 2

    def pair_copy(self, c):
        return remote(self.part.at[c, :, 1 - self.p.side], self.pair.at[c], self.dsem.at[0, c], self.dsem.at[1, c],
                      self.p.partner)

    def ring_copy(self, c, to_right, kind, chip, part):
        src = self.pair.at[c, chip, pl.ds(part * self.half, self.half), :]
        dst = (self.froml if to_right else self.fromr).at[c, kind]
        d = 0 if to_right else 1
        return remote(src, dst, self.rsem.at[0, d, kind, c], self.rsem.at[1, d, kind, c],
                      self.p.right if to_right else self.p.left)

    def run(self, compute, out, filler=None):
        p, half = self.p, self.half
        nchip = self.part.shape[1]
        sent = []

        def start(cp):
            cp.start()
            sent.append(cp)

        def produce(c):
            self.part[c] = compute(c).reshape(nchip, 2, self.rows, self.cols)
            start(self.pair_copy(c))

        def first(c):
            self.pair_copy(c).wait_recv()
            for chip in (p.ochip, p.rchip, p.lchip):
                self.pair[c, chip] = self.pair[c, chip] + self.part[c, chip, p.side]
                if chip is p.ochip:
                    start(self.ring_copy(c, True, 0, chip, 0))
                    start(self.ring_copy(c, False, 0, chip, 1))
                elif chip is p.rchip:
                    start(self.ring_copy(c, True, 1, chip, 1))
                else:
                    start(self.ring_copy(c, False, 1, chip, 0))

        def second(c):
            lo, hi = pl.ds(0, half), pl.ds(half, half)
            self.ring_copy(c, True, 0, p.ochip, 0).wait_recv()
            self.pair[c, p.rchip, lo, :] = self.pair[c, p.rchip, lo, :] + self.froml[c, 0]
            start(self.ring_copy(c, True, 2, p.rchip, 0))
            self.ring_copy(c, False, 0, p.ochip, 1).wait_recv()
            self.pair[c, p.lchip, hi, :] = self.pair[c, p.lchip, hi, :] + self.fromr[c, 0]
            start(self.ring_copy(c, False, 2, p.lchip, 1))

        def last(c):
            own = self.pair[c, p.chip] + self.part[c, p.chip, p.side]
            for d in (True, False):
                for kind in (1, 2):
                    self.ring_copy(c, d, kind, p.chip, 0).wait_recv()
            cs = pl.ds(c * self.cols, self.cols)
            out[0:half, cs] = own[0:half] + self.froml[c, 2] + self.fromr[c, 1]
            out[half:2 * half, cs] = own[half:2 * half] + self.froml[c, 1] + self.fromr[c, 2]

        for t in range(CHUNKS + 1):
            if t < CHUNKS:
                produce(t)
            if t >= 1:
                first(t - 1)
        if filler is not None:
            filler()
        for c in range(CHUNKS):
            second(c)
        for c in range(CHUNKS):
            last(c)
        for cp in sent:
            cp.wait_send()


def cols_loop(total, step, body):
    def one(i, carry):
        body(pl.multiple_of(i * step, step))
        return carry
    lax.fori_loop(0, total // step, one, 0)


def attention_forward(qkv, heads, o, prob=None):
    seq = qkv.shape[0]
    rows = lax.broadcasted_iota(jnp.int32, (seq, seq), 0)
    cols = lax.broadcasted_iota(jnp.int32, (seq, seq), 1)
    causal = rows >= cols
    for h in range(heads):
        at = h * 3 * HEAD_DIM
        q, k, v = (qkv[:, at + j * HEAD_DIM:at + (j + 1) * HEAD_DIM] for j in range(3))
        s = jnp.where(causal, dot_nt(q, k) * HEAD_DIM ** -0.5, -1e30)
        e = jnp.exp(s - jnp.max(s, axis=-1, keepdims=True))
        pr = e / jnp.sum(e, axis=-1, keepdims=True)
        if prob is not None:
            prob[h] = pr
        o[:, h * HEAD_DIM:(h + 1) * HEAD_DIM] = dot_nn(pr.astype(BF), v).astype(BF)


def attention_backward(qkv, heads, prob, d_heads, d_qkv):
    for h in range(heads):
        at = h * 3 * HEAD_DIM
        q, k, v = (qkv[:, at + j * HEAD_DIM:at + (j + 1) * HEAD_DIM] for j in range(3))
        do = d_heads[:, h * HEAD_DIM:(h + 1) * HEAD_DIM]
        pr = prob[h]
        dp = dot_nt(do, v)
        dv = dot_tn(pr.astype(BF), do)
        ds = (pr * (dp - jnp.sum(dp * pr, axis=-1, keepdims=True)) * HEAD_DIM ** -0.5).astype(BF)
        d_qkv[:, at:at + HEAD_DIM] = dot_nn(ds, k).astype(BF)
        d_qkv[:, at + HEAD_DIM:at + 2 * HEAD_DIM] = dot_tn(ds, q).astype(BF)
        d_qkv[:, at + 2 * HEAD_DIM:at + 3 * HEAD_DIM] = dv.astype(BF)


def sigmoid(x):
    return 1.0 / (1.0 + jnp.exp(-x))


def forward_kernel(n, layers, x, gain_a, gain_m, wq_h, wo_h, wg_h, wu_h, wd_h,
                   y, *rest):
    kept = rest[:layers - 1]
    (wq, wo, wg, wu, wd, ubuf, nbuf, qkv, o, mact, part, pair, froml, fromr, acc,
     wsem, us, ur, ns, nr, dsem, rsem) = rest[layers - 1:]
    place = Place(n)
    loads = []
    for l in range(layers):
        loads.append([])
        for j, (src, dst) in enumerate(((wq_h, wq), (wo_h, wo), (wg_h, wg), (wu_h, wu), (wd_h, wd))):
            cp = pltpu.make_async_copy(src.at[l], dst.at[l], wsem.at[l, j])
            cp.start()
            loads[l].append(cp)
    place.barrier()
    rows = x.shape[0]
    mine = pl.ds(pl.multiple_of(place.me * rows, rows), rows)
    heads = qkv.shape[1] // (3 * HEAD_DIM)
    scatter = Scatter(place, part, pair, froml, fromr, dsem, rsem)
    h = x[...]
    cc = part.shape[4]
    for l in range(layers):
        ubuf[mine, :] = norm(h, gain_a[l:l + 1, :])
        gather = Gather(place, ubuf, us, ur)
        gather.start()
        gather.finish()
        loads[l][0].wait()

        def qkv_cols(at):
            qkv[:, pl.ds(at, 256)] = dot_nn(ubuf[...], wq[l, :, pl.ds(at, 256)]).astype(BF)
        cols_loop(qkv.shape[1], 256, qkv_cols)
        attention_forward(qkv, heads, o)
        loads[l][1].wait()
        scatter.run(lambda c: dot_nn(o[...], wo[l, :, c * cc:(c + 1) * cc]), acc)
        h1 = h + acc[...].astype(BF)
        nbuf[mine, :] = norm(h1, gain_m[l:l + 1, :])
        gather = Gather(place, nbuf, ns, nr)
        gather.start()
        loads[l][2].wait()
        loads[l][3].wait()
        gather.finish()

        def mlp_cols(at):
            cs = pl.ds(at, 256)
            z1 = dot_nn(nbuf[...], wg[l, :, cs]).astype(BF).astype(F32)
            z3 = dot_nn(nbuf[...], wu[l, :, cs]).astype(BF).astype(F32)
            mact[:, cs] = (z1 * sigmoid(z1) * z3).astype(BF)
        cols_loop(mact.shape[1], 256, mlp_cols)
        loads[l][4].wait()
        scatter.run(lambda c: dot_nn(mact[...], wd[l, :, c * cc:(c + 1) * cc]), acc)
        h = h1 + acc[...].astype(BF)
        if l < layers - 1:
            kept[l][...] = h
    y[...] = h


def backward_kernel(n, l, others, share, hin, dout, gain_a, gain_m, wq_h, wo_h, wg_h, wu_h, wd_h, *rest):
    gains_in = None
    if others:
        gains_in, rest = rest[0], rest[1:]
    (dx, gains, u_h, n_h, do_h, da_h, o_h, m_h, dg_h, du_h, dqkv_h,
     wq, wo, wg, wu, wd, ubuf, nbuf, dobuf, dabuf, qkv, o, prob, mact, dgate, dup, dgated, dheads, dqkv,
     part, pair, froml, fromr, acc,
     wsem, osem, us, ur, ns, nr, dos, dor, das, dar, dsem, rsem, gs, gr) = rest
    place = Place(n)
    loads = []
    for j, (src, dst) in enumerate(((wq_h, wq), (wo_h, wo), (wd_h, wd), (wg_h, wg), (wu_h, wu))):
        cp = pltpu.make_async_copy(src.at[l], dst, wsem.at[j])
        cp.start()
        loads.append(cp)
    place.barrier(everyone=share)
    stores = []

    def store(src, dst):
        cp = pltpu.make_async_copy(src, dst, osem.at[len(stores)])
        cp.start()
        stores.append(cp)

    rows = hin.shape[0]
    mine = pl.ds(pl.multiple_of(place.me * rows, rows), rows)
    heads = qkv.shape[1] // (3 * HEAD_DIM)
    scatter = Scatter(place, part, pair, froml, fromr, dsem, rsem)
    cc = part.shape[4]
    ga, gm = gain_a[l:l + 1, :], gain_m[l:l + 1, :]

    h = hin[...]
    ubuf[mine, :] = norm(h, ga)
    gu = Gather(place, ubuf, us, ur)
    gu.start()
    dobuf[mine, :] = dout[...]
    gd = Gather(place, dobuf, dos, dor)
    gd.start()
    gu.finish()
    loads[0].wait()

    def qkv_cols(at):
        qkv[:, pl.ds(at, 256)] = dot_nn(ubuf[...], wq[:, pl.ds(at, 256)]).astype(BF)
    cols_loop(qkv.shape[1], 256, qkv_cols)
    attention_forward(qkv, heads, o, prob)
    gd.finish()
    store(ubuf, u_h)
    store(o, o_h)
    store(dobuf, do_h)
    loads[1].wait()
    loads[2].wait()

    def gated_cols():
        def body(at):
            dgated[:, pl.ds(at, 256)] = dot_nt(dobuf[...], wd[pl.ds(at, 256), :])
        cols_loop(dgated.shape[1], 256, body)
    scatter.run(lambda c: dot_nn(o[...], wo[:, c * cc:(c + 1) * cc]), acc, gated_cols)
    h1 = h + acc[...].astype(BF)
    nbuf[mine, :] = norm(h1, gm)
    gn = Gather(place, nbuf, ns, nr)
    gn.start()
    loads[3].wait()
    loads[4].wait()
    gn.finish()
    store(nbuf, n_h)

    def mlp_cols(at):
        cs = pl.ds(at, 256)
        z1 = dot_nn(nbuf[...], wg[:, cs]).astype(BF).astype(F32)
        z3 = dot_nn(nbuf[...], wu[:, cs]).astype(BF).astype(F32)
        sg = sigmoid(z1)
        act = z1 * sg
        mact[:, cs] = (act * z3).astype(BF)
        dm = dgated[:, cs].astype(BF).astype(F32)
        dup[:, cs] = (dm * act).astype(BF)
        dgate[:, cs] = (dm * z3 * (sg * (1.0 + z1 * (1.0 - sg)))).astype(BF)
    cols_loop(mact.shape[1], 256, mlp_cols)
    store(mact, m_h)
    store(dgate, dg_h)
    store(dup, du_h)

    scatter.run(lambda c: dot_nt(dgate[...], wg[c * cc:(c + 1) * cc, :]) + dot_nt(dup[...], wu[c * cc:(c + 1) * cc, :]), acc)
    d_norm, dgain_m = norm_grad(h1, gm, acc[...].astype(BF))
    d_h1 = dout[...] + d_norm
    dabuf[mine, :] = d_h1
    gda = Gather(place, dabuf, das, dar)
    gda.start()
    gda.finish()
    store(dabuf, da_h)

    def heads_cols(at):
        dheads[:, pl.ds(at, 128)] = dot_nt(dabuf[...], wo[pl.ds(at, 128), :]).astype(BF)
    cols_loop(dheads.shape[1], 128, heads_cols)
    attention_backward(qkv, heads, prob, dheads, dqkv)
    store(dqkv, dqkv_h)
    scatter.run(lambda c: dot_nt(dqkv[...], wq[c * cc:(c + 1) * cc, :]), acc)
    d_norm, dgain_a = norm_grad(h, ga, acc[...].astype(BF))
    dx[...] = d_h1 + d_norm
    if share:
        me = place.me
        if others:
            gains[me, 2:, :] = gains_in[...]
        gains[me, 0:1, :] = dgain_a
        gains[me, 1:2, :] = dgain_m
        cps = []
        for k in range(1, n):
            cp = remote(gains.at[me], gains.at[me], gs.at[k], gr.at[k], lax.rem(me + k, n))
            cp.start()
            cps.append(cp)
        for k in range(1, n):
            src = lax.rem(me + n - k, n)
            remote(gains.at[src], gains.at[src], gs.at[k], gr.at[k], place.partner).wait_recv()
        for cp in cps:
            cp.wait_send()
    else:
        k = 0
        if others:
            gains[2:, :] = gains_in[...]
        gains[0:1, :] = dgain_a
        gains[1:2, :] = dgain_m
    for cp in stores:
        cp.wait()


def weight_kernel(last, *refs):
    refs = list(refs)
    u, nn, do, da, o, m, dg, du, dqkv = refs[:9]
    refs = refs[9:]
    if last:
        y, dx, gains = refs[:3]
        refs = refs[3 + 5:]
        gq, go, gg, gu, gd, y_o, dx_o, ga_o, gm_o = refs
    else:
        gq, go, gg, gu, gd = refs
    gq[0] = dot_tn(u[...], dqkv[...]).astype(BF)
    go[0] = dot_tn(o[...], da[...]).astype(BF)
    gg[0] = dot_tn(nn[...], dg[...]).astype(BF)
    gu[0] = dot_tn(nn[...], du[...]).astype(BF)
    gd[0] = dot_tn(m[...], do[...]).astype(BF)
    if last:
        @pl.when(pl.program_id(0) == 0)
        def _():
            y_o[...] = y[...]
            dx_o[...] = dx[...]
            total = gains[0]
            for k in range(1, gains.shape[0]):
                total = total + gains[k]
            for j in range(ga_o.shape[0]):
                ga_o[j:j + 1, :] = total[2 * j:2 * j + 1, :]
                gm_o[j:j + 1, :] = total[2 * j + 1:2 * j + 2, :]


def solution(mesh):
    n = mesh.shape['tp']
    row_spec = P(('dp', 'tp'), None)
    col_spec = P(None, None, 'tp')
    mid_spec = P(None, 'tp', None)
    in_specs = (row_spec, row_spec, P(None, None), P(None, None), col_spec, mid_spec, col_spec, col_spec, mid_spec)
    out_specs = (row_spec, row_spec, P('dp', None, 'tp'), P('dp', 'tp', None), P('dp', None, 'tp'), P('dp', None, 'tp'), P('dp', 'tp', None), P('dp', None), P('dp', None))
    vm = pl.BlockSpec(memory_space=pltpu.VMEM)
    hbm = pl.BlockSpec(memory_space=pl.ANY)
    DMA = pltpu.SemaphoreType.DMA

    def step(x, grad_y, gain_attn, gain_mlp, w_qkv, w_out, w_gate, w_up, w_down):
        layers, d, qcols = w_qkv.shape
        ocols = w_out.shape[1]
        ff = w_gate.shape[2]
        rows = x.shape[0]
        seq = rows * n
        heads = qcols // (3 * HEAD_DIM)
        cc = d // CHUNKS
        nchip = n // 2
        weights = (w_qkv, w_out, w_gate, w_up, w_down)
        shard = jax.ShapeDtypeStruct((rows, d), BF)

        def comm_scratch():
            return [
                pltpu.VMEM((CHUNKS, nchip, 2, rows, cc), F32),
                pltpu.VMEM((CHUNKS, nchip, rows, cc), F32),
                pltpu.VMEM((CHUNKS, 3, rows // 2, cc), F32),
                pltpu.VMEM((CHUNKS, 3, rows // 2, cc), F32),
                pltpu.VMEM((rows, d), F32),
            ]

        def wscratch(*lead):
            return [pltpu.VMEM((*lead, *w.shape[1:]), BF) for w in weights]

        full = pltpu.VMEM((seq, d), BF)
        fwd = pl.pallas_call(
            functools.partial(forward_kernel, n, layers),
            out_shape=[shard] * layers,
            in_specs=[vm] * 3 + [hbm] * 5,
            out_specs=[vm] * layers,
            scratch_shapes=wscratch(layers) + [full, full, pltpu.VMEM((seq, qcols), BF), pltpu.VMEM((seq, ocols), BF),
                                               pltpu.VMEM((seq, ff), BF)] + comm_scratch()
            + [DMA((layers, 5))] + [DMA((13,))] * 4 + [DMA((2, CHUNKS)), DMA((2, 2, 3, CHUNKS))],
            compiler_params=pltpu.CompilerParams(collective_id=0, has_side_effects=True, vmem_limit_bytes=VMEM_LIMIT),
            name='fwd',
        )(x, gain_attn, gain_mlp, *weights)
        y = fwd[0]
        layer_in = [x] + list(fwd[1:])
        d_hidden = grad_y
        grads = None
        gains = None
        gshapes = [jax.ShapeDtypeStruct(w.shape, BF) for w in weights]
        for l in reversed(range(layers)):
            done = layers - 1 - l
            share = l == 0
            gshape = (2 * (done + 1), d)
            res = [((seq, d), BF)] * 4 + [((seq, ocols), BF)] + [((seq, ff), BF)] * 3 + [((seq, qcols), BF)]
            gsem = [DMA((n,)), DMA((n,))]
            out = pl.pallas_call(
                functools.partial(backward_kernel, n, l, done > 0, share),
                out_shape=[shard, jax.ShapeDtypeStruct(((n,) if share else ()) + gshape, F32)]
                + [jax.ShapeDtypeStruct(s, t) for s, t in res],
                in_specs=[vm] * 4 + [hbm] * 5 + ([vm] if done else []),
                out_specs=[vm] * 2 + [hbm] * 9,
                scratch_shapes=wscratch() + [full] * 4 + [
                    pltpu.VMEM((seq, qcols), BF), pltpu.VMEM((seq, ocols), BF), pltpu.VMEM((heads, seq, seq), F32),
                    pltpu.VMEM((seq, ff), BF), pltpu.VMEM((seq, ff), BF), pltpu.VMEM((seq, ff), BF),
                    pltpu.VMEM((seq, ff), F32), pltpu.VMEM((seq, ocols), BF), pltpu.VMEM((seq, qcols), BF),
                ] + comm_scratch() + [DMA((5,)), DMA((9,))] + [DMA((13,))] * 8
                + [DMA((2, CHUNKS)), DMA((2, 2, 3, CHUNKS))] + gsem,
                compiler_params=pltpu.CompilerParams(collective_id=1 + done, has_side_effects=True,
                                                     vmem_limit_bytes=VMEM_LIMIT),
                name=f'bwd{l}',
            )(layer_in[l], d_hidden, gain_attn, gain_mlp, *weights, *([gains] if done else []))
            d_hidden, gains = out[0], out[1]
            u, nn, do, da, o, m, dg, du, dqkv = out[2:]
            steps = d // 256
            ins = [
                (u, pl.BlockSpec((seq, 256), lambda i: (0, i))),
                (nn, pl.BlockSpec((seq, 256), lambda i: (0, i))),
                (do, pl.BlockSpec((seq, d), lambda i: (0, 0))),
                (da, pl.BlockSpec((seq, 256), lambda i: (0, i))),
                (o, pl.BlockSpec((seq, ocols), lambda i: (0, 0))),
                (m, pl.BlockSpec((seq, ff // steps), lambda i: (0, i))),
                (dg, pl.BlockSpec((seq, ff), lambda i: (0, 0))),
                (du, pl.BlockSpec((seq, ff), lambda i: (0, 0))),
                (dqkv, pl.BlockSpec((seq, qcols), lambda i: (0, 0))),
            ]
            outs = [
                pl.BlockSpec((1, 256, qcols), lambda i, l=l: (l, i, 0)),
                pl.BlockSpec((1, ocols, 256), lambda i, l=l: (l, 0, i)),
                pl.BlockSpec((1, 256, ff), lambda i, l=l: (l, i, 0)),
                pl.BlockSpec((1, 256, ff), lambda i, l=l: (l, i, 0)),
                pl.BlockSpec((1, ff // steps, d), lambda i, l=l: (l, i, 0)),
            ]
            oshape = list(gshapes)
            alias = {}
            whole = lambda a: pl.BlockSpec(a.shape, lambda i: (0,) * len(a.shape))
            if share:
                ins += [(a, whole(a)) for a in (y, d_hidden, gains)]
                gsum = jax.ShapeDtypeStruct((layers, d), F32)
                oshape += [shard, shard, gsum, gsum]
                outs += [whole(s) for s in (shard, shard, gsum, gsum)]
            if grads is not None:
                alias = {len(ins) + j: j for j in range(5)}
                ins += [(g, hbm) for g in grads]
            grads = pl.pallas_call(
                functools.partial(weight_kernel, share),
                grid=(steps,),
                out_shape=oshape,
                in_specs=[s for _, s in ins],
                out_specs=outs,
                input_output_aliases=alias,
                compiler_params=pltpu.CompilerParams(dimension_semantics=('arbitrary',)),
                name=f'wgrad{l}',
            )(*[a for a, _ in ins])
        gq, go, gg, gu, gd, y, d_hidden, gsa, gsm = grads
        return (y, d_hidden, gq, go, gg, gu, gd, gsa, gsm)

    return jax.shard_map(step, mesh=mesh, in_specs=in_specs, out_specs=out_specs, check_vma=False)
```

time: 684 us -> 312 us (0.46)
  waiting for transfers between devices: 447 us -> 0 us
  Pallas kernels: 0 us -> 309 us
  matrix products: 130 us -> 0 us
  other arithmetic: 52.8 us -> 0 us
  blocking collectives: 24 us -> 0 us
  between operations: 16 us -> 0.85 us
    pallas_call x0 -> x5, Pallas kernels: none -> 309 us  [the longest x2 179 us: step(): pl.pallas_call(functools.partial(backward_kernel, n, l, done > 0, share),...]
    reduce_scatter x10 -> x0, waiting for transfers between devices: 241 us -> none  [scatter_rows(): lax.psum_scatter(part_sum, 'tp', scatter_dimension=0, tiled=True)]
    all_gather x12 -> x0, waiting for transfers between devices: 203 us -> none  [gather_rows(): return lax.all_gather(row_shard, 'tp', axis=0, tiled=True)]
    dot_general x52 -> x0, matrix products: 130 us -> none  [the longest x36 70.9 us: contract(): jnp.einsum(eq_form, left_op, right_op, preferred_element_type=jnp.float32)]
    psum x1 -> x0, blocking collectives: 24 us -> none  [device_step(): gain_grads = lax.psum(jnp.stack([stacked[0], stacked[1]]), 'tp')]
    another operation x8 -> x0, other arithmetic: 23 us -> none  [the longest x4 22.7 us: device_step(): jnp.stack([grads[kind_idx] for grads in layer_grads])]
    reduce_sum x16 -> x0, other arithmetic: 14 us -> none  [the longest x8 7.32 us: rms_norm(): jnp.mean(hidden_f * hidden_f, axis=-1, keepdims=True) + NORM_EPS]
    add x5 -> x0, other arithmetic: 8.65 us -> none  [the longest x2 3.51 us: layer_backward(): d_hidden_mid + d_norm_in]
  transfers between devices with their start and end apart: 22 -> 0, of which waited for: 20 -> 0; matrix products, arithmetic and copies ran while one was open for 17% -> 0% of each run, Pallas kernels for 0% -> 0%
where the time goes in v1:
time: 312 us; the launch traced here: 310 us
  Pallas kernels  309 us (99%)
    pallas_call x2, Pallas kernels, step(): pl.pallas_call(functools.partial(backward_kernel, n, l, done > 0, share),...  179 us
    pallas_call x1, Pallas kernels, step(): pl.pallas_call(functools.partial(forward_kernel, n, layers), out_shape=[s...  106 us
    pallas_call x2, Pallas kernels, step(): pl.pallas_call(functools.partial(weight_kernel, share), grid=(steps,), ou...  24.1 us

profile of v1, /device:TPU:88, one launch (start us, length us, event | category | flops | bytes accessed | tf_op | source)
XLA Modules:
  0.0 310.3 jit_solution(16690416077003920749)
XLA Ops:
  0.6 106.2 %fwd.1 = (bf16[32,2048]{1,0:T(8,128)(2,1)}, bf16[32,2048]{1,0:T(8,128)(2,1)}) custom-call(bf16[32,2048]{1,0:T(8,128)(2,1)} %hin.1, f32[2,2048]{1,0:T(2,128)} %gain_a.5, f32[2,2048]{1,0:T(2,128)} %gain_m.5, bf16[2,2048,768]{2,1,0:T(8,128)(2,1)} %wq_h.5, bf16[2,256,2048]{2,1,0:T(8,128)(2,1)} %wo_h.5, bf16[2,2048,1024]{2,1,0:T(8,128)(2,1)} %wg_h.5, ...), custom_call_target="tpu_custom_call" | custom-call | tf_op jit(solution)/shard_map/fwd/pallas_call | solution.py:500
  106.9 86.5 %bwd1.1 = (bf16[32,2048]{1,0:T(8,128)(2,1)}, f32[2,2048]{1,0:T(2,128)}, bf16[256,2048]{1,0:T(8,128)(2,1)}, bf16[256,2048]{1,0:T(8,128)(2,1)}, bf16[256,2048]{1,0...) custom-call(bf16[32,2048]{1,0:T(8,128)(2,1)} %get-tuple-element.47.h, ...), custom_call_target="tpu_custom_call" | custom-call | tf_op jit(solution)/shard_map/bwd1/pallas_call | solution.py:523
  193.4 92.6 %bwd0.1 = (bf16[32,2048]{1,0:T(8,128)(2,1)}, f32[8,4,2048]{2,1,0:T(4,128)}, bf16[256,2048]{1,0:T(8,128)(2,1)}, bf16[256,2048]{1,0:T(8,128)(2,1)}, bf16[256,2048]...) custom-call(bf16[32,2048]{1,0:T(8,128)(2,1)} %hin.1, ...), custom_call_target="tpu_custom_call" | custom-call | tf_op jit(solution)/shard_map/bwd0/pallas_call | solution.py:523
  286.0 11.6 %wgrad1.1 = (bf16[2,2048,768]{2,1,0:T(8,128)(2,1)}, bf16[2,256,2048]{2,1,0:T(8,128)(2,1)}, bf16[2,2048,1024]{2,1,0:T(8,128)(2,1)}, bf16[2,2048,1024]{2,1,0:T(8,128)(2,1)}, bf16[2,1024,2048]{2,1,0:T(8,128)(2,1)}) custom-call(bf16[256,2048]{1,0:T(8,128)(2,1)} %get-tuple-element.62.refs_0_, bf16[256,2048]{1,0:T(8,128)(2,1)} %get-tuple-element.63.refs_1_, ...), custom_call_target="tpu_custom_call" | custom-call | tf_op jit(solution)/shard_map/wgrad1/pallas_call | solution.py:571
  297.6 12.5 %wgrad0.1 = (bf16[2,2048,768]{2,1,0:T(8,128)(2,1)}, bf16[2,256,2048]{2,1,0:T(8,128)(2,1)}, bf16[2,2048,1024]{2,1,0:T(8,128)(2,1)}, bf16[2,2048,1024]{2,1,0:T(8,1...) custom-call(bf16[256,2048]{1,0:T(8,128)(2,1)} %get-tuple-element.50., ...), custom_call_target="tpu_custom_call", output_to_operand_aliasing={{0}: (12, {}), {1}: (13, {}), {2}: (14, {}), {3}: (15, {}),... | custom-call | tf_op jit(solution)/shard_map/wgrad0/pallas_call | solution.py:571
